TPU v7x, 32 devices: a whole 2x2x4 slice. The times are simulated.
32 devices in a mesh: book: 4 (over y, core), path: 8 (over z, x).
Axes of the slice: x: 2, y: 2, z: 4, core: 2. Of those that a mesh axis runs over, the one named last changes fastest.
Arguments:
- states: float32 [10, 20, 65536], P(None, None, ('book', 'path')), parts along dimension 2, may hold values from -7.5 to 7.5
- itm_flags: int32 [10, 65536], P(None, ('book', 'path')), parts along dimension 1, may hold values 0 or 1
- terminal: float32 [65536], P(('book', 'path')), parts along dimension 0, may hold values from -3.5 to 5.5
- strike: float32 [4], P('book'), parts along dimension 0, may hold values from 0.025 to 0.035
- date_index: int32 [65536], P(('book', 'path')), parts along dimension 0, may hold values from 0 to 9
Outputs:
- cash_flow: float32 [65536], P(('book', 'path')), parts along dimension 0
- book_price: float32 [4], P('book'), parts along dimension 0
- coefficients: float32 [40, 231], P('book'), parts along dimension 0
There are 4 independent parts, one for each index of `book`. A program takes and returns all parts, laid end to end along the dimension named above; each array names one. Nothing has to cross between parts.
All inputs are finite; a program needn't handle non-finite values. No bound on the sum of `itm_flags` on one device may be relied on, other than what follows from the above.
Results may differ from a plain program's by a relative error of at most 0.0003.
Values sent between devices are 32-bit elements; how exact they have to be, the bound alone decides.
A program may use at most 192 MiB of HBM per device.

v0:
```python
import jax
import jax.numpy as jnp
import numpy as np
from jax import lax
from jax.sharding import PartitionSpec as P

ridge_weight = 0.05
temper_scale = 0.5
highest = lax.Precision.HIGHEST


def swap_terms(factors, strike_level):
    forwards = 0.03 * jnp.exp(0.25 * factors)
    discount = jnp.cumprod(1.0 / (1.0 + 0.25 * forwards), axis=0)
    annuity = 0.25 * jnp.sum(discount, axis=0)
    swap_rate = (1.0 - discount[-1]) / annuity
    return (100.0 * annuity * (swap_rate - strike_level), discount[0])


def basis_of(scaled, pair_left, pair_right):
    ones_row = jnp.ones((1, scaled.shape[1]), jnp.float32)
    return jnp.concatenate([ones_row, scaled, scaled[pair_left] * scaled[pair_right]], axis=0)


def gram_only(basis_rows, money_flags):
    weighted = basis_rows * money_flags
    return lax.dot_general(
        weighted,
        basis_rows,
        (((1,), (1,)), ((), ())),
        precision=highest,
        preferred_element_type=jnp.float32,
    )


def system_of(gram_sums, path_count):
    return gram_sums / path_count + ridge_weight * jnp.eye(gram_sums.shape[0], dtype=jnp.float32)


def shards(states, itm_flags, terminal, strike, date_index):
    date_count, factor_count, local_paths = states.shape
    pair_left, pair_right = np.triu_indices(factor_count)
    total_paths = local_paths * lax.axis_size("path")
    value_now = terminal
    coef_list = []
    money_all = itm_flags.astype(jnp.float32)
    count_all, first_all, second_all = lax.psum(
        (
            jnp.sum(money_all, axis=1),
            jnp.sum(money_all[:, None, :] * states, axis=2),
            jnp.sum(money_all[:, None, :] * states * states, axis=2),
        ),
        "path",
    )
    mean_all = first_all / count_all[:, None]
    scale_all = jnp.sqrt(second_all / count_all[:, None] - mean_all * mean_all + 1e-05)
    local_list = []
    for date_step in range(date_count):
        scaled = (states[date_step] - mean_all[date_step][:, None]) / scale_all[date_step][:, None]
        local_list.append(gram_only(basis_of(scaled, pair_left, pair_right), money_all[date_step]))
    gram_stack = lax.psum(jnp.stack(local_list, axis=0), "path")
    chol_list = [
        jnp.linalg.cholesky(system_of(gram_stack[date_step], count_all[date_step]))
        for date_step in range(date_count)
    ]
    for date_step in range(date_count - 1, -1, -1):
        factors = states[date_step]
        exercise, discount = swap_terms(factors, strike[0])
        value_now = value_now * discount
        money_flags = money_all[date_step]
        scaled = (factors - mean_all[date_step][:, None]) / scale_all[date_step][:, None]
        basis_rows = basis_of(scaled, pair_left, pair_right)
        rhs_local = jnp.dot(
            basis_rows * money_flags,
            value_now,
            precision=highest,
            preferred_element_type=jnp.float32,
        )
        rhs_total = lax.psum(rhs_local, "path")
        coef_vector = jax.scipy.linalg.cho_solve(
            (chol_list[date_step], True), rhs_total / count_all[date_step]
        )
        continuation = jnp.dot(
            coef_vector, basis_rows, precision=highest, preferred_element_type=jnp.float32
        )
        open_date = (date_index <= date_step).astype(jnp.float32)
        weights = jax.nn.sigmoid((exercise - continuation) / temper_scale) * money_flags * open_date
        value_now = value_now + weights * (exercise - value_now)
        coef_list.append(coef_vector)
    book_sum = lax.psum(jnp.sum(value_now), "path")
    book_price = jnp.reshape(book_sum / total_paths, (1,))
    return (value_now, book_price, jnp.stack(coef_list[::-1], axis=0))


def solution(mesh):
    in_specs = (
        P(None, None, ("book", "path")),
        P(None, ("book", "path")),
        P(("book", "path")),
        P("book"),
        P(("book", "path")),
    )
    out_specs = (P(("book", "path")), P("book"), P("book", None))
    return jax.shard_map(shards, mesh=mesh, in_specs=in_specs, out_specs=out_specs, check_vma=False)
```

profile of v0, /device:TPU:0, one launch (start us, length us, event | category | flops | bytes accessed | tf_op | source)
XLA Modules:
  0.0 1180.8 jit_solution(16946577159541569556)
XLA Ops:
  11.4 38.8 %all-reduce.3 = (f32[10,20]{1,0:T(8,128)S(1)}, f32[10]{0:T(128)S(1)}, f32[10,20]{1,0:T(8,128)S(1)}) all-reduce(f32[10,20]{1,0:T(8,128)S(1)} %get-tuple-element.80, f32[10]{0:T(128)S(1)} %convert_reduce_fusion, f32[10,20]{1,0:T(8,128)S(1)} %get-tuple-element.79), channel_id=1, replica_groups=mesh['book'=4,'path'=8] {'path'}, use_global_device_ids=true, to_apply=%region_7.8 | all-reduce | flops 410 | bytes 3280 | tf_op jit(solution)/shard_map/psum | solution.py:47
  175.2 17.8 %psum.109 = f32[231]{0:T(256)S(1)} all-reduce(f32[231]{0:T(256)S(1)} %bitcast.1074), channel_id=1, replica_groups=mesh['book'=4,'path'=8] {'path'}, use_global_device_ids=true, to_apply=%region_13.15 | all-reduce | flops 231 | bytes 1848 | tf_op jit(solution)/shard_map/psum | solution.py:79
  197.4 67.7 %all-reduce.6.cloned.1.call-done = f32[10,231,231]{1,2,0:T(8,128)} async-done(((f32[10,231,231]{1,2,0:T(8,128)}), f32[10,231,231]{1,2,0:T(8,128)}) %all-reduce.6.cloned.1.call-update) | async-done | bytes 2134456 | tf_op jit(solution)/shard_map/psum | solution.py:61
  268.5 11.7 cholesky.504
  280.9 9.8 custom-call.31
  291.2 9.4 cholesky.524
  302.9 19.8 %custom-call.32 = f32[2,128,128]{1,2,0:T(8,128)S(1)} custom-call(f32[2,128,128]{2,1,0:T(8,128)S(1)} %pad_maximum_fusion.10), custom_call_target="InvertDiagBlocksLowerTriangular" | custom-call | tf_op jit(solution)/shard_map/jit(_cho_solve)/triangular_solve | solution.py:80
  338.4 12.5 %cholesky.846 = f32[128,128]{1,0:T(8,128)S(1)} custom-call(f32[128,128]{1,0:T(8,128)} %cholesky.907), custom_call_target="Cholesky" | custom-call | tf_op jit(solution)/shard_map/jit(cholesky)/cholesky | solution.py:63
  353.0 10.6 custom-call.49
  385.0 12.7 %cholesky.808 = f32[128,128]{1,0:T(8,128)S(1)} custom-call(f32[128,128]{1,0:T(8,128)} %cholesky.904), custom_call_target="Cholesky" | custom-call | tf_op jit(solution)/shard_map/jit(cholesky)/cholesky | solution.py:63
  399.9 10.6 custom-call.47
  430.1 11.7 cholesky.770
  443.7 9.8 custom-call.45
  471.4 11.7 cholesky.732
  484.6 9.8 custom-call.43
  497.1 9.6 cholesky.752
  511.7 11.7 cholesky.694
  524.8 9.8 custom-call.41
  535.8 9.4 cholesky.714
  550.3 11.9 %cholesky.656 = f32[128,128]{1,0:T(8,128)S(1)} custom-call(f32[128,128]{1,0:T(8,128)S(1)} %cholesky.892), custom_call_target="Cholesky" | custom-call | tf_op jit(solution)/shard_map/jit(cholesky)/cholesky | solution.py:63
  563.6 9.8 custom-call.39
  589.1 12.1 %cholesky.618 = f32[128,128]{1,0:T(8,128)S(1)} custom-call(f32[128,128]{1,0:T(8,128)S(1)} %cholesky.889), custom_call_target="Cholesky" | custom-call | tf_op jit(solution)/shard_map/jit(cholesky)/cholesky | solution.py:63
  602.6 9.8 custom-call.37
  613.5 9.4 cholesky.638
  627.9 11.7 cholesky.580
  641.0 9.8 custom-call.35
  667.8 13.2 %cholesky.542 = f32[128,128]{1,0:T(8,128)} custom-call(f32[128,128]{1,0:T(8,128)} %cholesky.883), custom_call_target="Cholesky" | custom-call | tf_op jit(solution)/shard_map/jit(cholesky)/cholesky | solution.py:63
  684.7 11.3 custom-call.33
  699.3 10.8 cholesky.562
  719.7 19.5 %psum.110 = f32[231]{0:T(256)S(1)} all-reduce(f32[231]{0:T(256)} %bitcast.1075), channel_id=1, replica_groups=mesh['book'=4,'path'=8] {'path'}, use_global_device_ids=true, to_apply=%region_16.19 | all-reduce | flops 231 | bytes 1848 | tf_op jit(solution)/shard_map/psum | solution.py:79
  744.1 21.1 %custom-call.34 = f32[2,128,128]{1,2,0:T(8,128)} custom-call(f32[2,128,128]{2,1,0:T(8,128)} %pad_maximum_fusion.11), custom_call_target="InvertDiagBlocksLowerTriangular" | custom-call | tf_op jit(solution)/shard_map/jit(_cho_solve)/triangular_solve | solution.py:80
  775.7 20.5 %custom-call.36 = f32[2,128,128]{1,2,0:T(8,128)S(1)} custom-call(f32[2,128,128]{2,1,0:T(8,128)} %pad_maximum_fusion.12), custom_call_target="InvertDiagBlocksLowerTriangular" | custom-call | tf_op jit(solution)/shard_map/jit(_cho_solve)/triangular_solve | solution.py:80
  800.6 18.2 %psum.111 = f32[231]{0:T(256)} all-reduce(f32[231]{0:T(256)} %bitcast.1076), channel_id=1, replica_groups=mesh['book'=4,'path'=8] {'path'}, use_global_device_ids=true, to_apply=%region_19.22 | all-reduce | flops 231 | bytes 1848 | tf_op jit(solution)/shard_map/psum | solution.py:79
  826.7 19.7 %custom-call.38 = f32[2,128,128]{1,2,0:T(8,128)S(1)} custom-call(f32[2,128,128]{2,1,0:T(8,128)S(1)} %pad_maximum_fusion.13), custom_call_target="InvertDiagBlocksLowerTriangular" | custom-call | tf_op jit(solution)/shard_map/jit(_cho_solve)/triangular_solve | solution.py:80
  850.2 19.2 %psum.112 = f32[231]{0:T(256)S(1)} all-reduce(f32[231]{0:T(256)S(1)} %bitcast.1077), channel_id=1, replica_groups=mesh['book'=4,'path'=8] {'path'}, use_global_device_ids=true, to_apply=%region_22.25 | all-reduce | flops 231 | bytes 1848 | tf_op jit(solution)/shard_map/psum | solution.py:79
  876.1 19.7 %custom-call.40 = f32[2,128,128]{1,2,0:T(8,128)S(1)} custom-call(f32[2,128,128]{2,1,0:T(8,128)S(1)} %pad_maximum_fusion.14), custom_call_target="InvertDiagBlocksLowerTriangular" | custom-call | tf_op jit(solution)/shard_map/jit(_cho_solve)/triangular_solve | solution.py:80
  899.1 17.4 %psum.113 = f32[231]{0:T(256)S(1)} all-reduce(f32[231]{0:T(256)S(1)} %bitcast.1078), channel_id=1, replica_groups=mesh['book'=4,'path'=8] {'path'}, use_global_device_ids=true, to_apply=%region_25.28 | all-reduce | flops 231 | bytes 1848 | tf_op jit(solution)/shard_map/psum | solution.py:79
  922.6 19.7 %custom-call.42 = f32[2,128,128]{1,2,0:T(8,128)S(1)} custom-call(f32[2,128,128]{2,1,0:T(8,128)S(1)} %pad_maximum_fusion.15), custom_call_target="InvertDiagBlocksLowerTriangular" | custom-call | tf_op jit(solution)/shard_map/jit(_cho_solve)/triangular_solve | solution.py:80
  944.1 19.2 %psum.114 = f32[231]{0:T(256)S(1)} all-reduce(f32[231]{0:T(256)S(1)} %bitcast.1079), channel_id=1, replica_groups=mesh['book'=4,'path'=8] {'path'}, use_global_device_ids=true, to_apply=%region_28.31 | all-reduce | flops 231 | bytes 1848 | tf_op jit(solution)/shard_map/psum | solution.py:79
  969.3 19.7 %custom-call.44 = f32[2,128,128]{1,2,0:T(8,128)S(1)} custom-call(f32[2,128,128]{2,1,0:T(8,128)S(1)} %pad_maximum_fusion.16), custom_call_target="InvertDiagBlocksLowerTriangular" | custom-call | tf_op jit(solution)/shard_map/jit(_cho_solve)/triangular_solve | solution.py:80
  990.8 17.5 %psum.115 = f32[231]{0:T(256)S(1)} all-reduce(f32[231]{0:T(256)S(1)} %bitcast.1080), channel_id=1, replica_groups=mesh['book'=4,'path'=8] {'path'}, use_global_device_ids=true, to_apply=%region_31.34 | all-reduce | flops 231 | bytes 1848 | tf_op jit(solution)/shard_map/psum | solution.py:79
  1014.4 19.7 %custom-call.46 = f32[2,128,128]{1,2,0:T(8,128)S(1)} custom-call(f32[2,128,128]{2,1,0:T(8,128)S(1)} %pad_maximum_fusion.17), custom_call_target="InvertDiagBlocksLowerTriangular" | custom-call | tf_op jit(solution)/shard_map/jit(_cho_solve)/triangular_solve | solution.py:80
  1035.9 19.2 %psum.116 = f32[231]{0:T(256)S(1)} all-reduce(f32[231]{0:T(256)S(1)} %bitcast.1081), channel_id=1, replica_groups=mesh['book'=4,'path'=8] {'path'}, use_global_device_ids=true, to_apply=%region_34.37 | all-reduce | flops 231 | bytes 1848 | tf_op jit(solution)/shard_map/psum | solution.py:79
  1061.2 19.7 %custom-call.48 = f32[2,128,128]{1,2,0:T(8,128)S(1)} custom-call(f32[2,128,128]{2,1,0:T(8,128)S(1)} %pad_maximum_fusion.18), custom_call_target="InvertDiagBlocksLowerTriangular" | custom-call | tf_op jit(solution)/shard_map/jit(_cho_solve)/triangular_solve | solution.py:80
  1082.7 17.5 %psum.117 = f32[231]{0:T(256)S(1)} all-reduce(f32[231]{0:T(256)S(1)} %bitcast.1082), channel_id=1, replica_groups=mesh['book'=4,'path'=8] {'path'}, use_global_device_ids=true, to_apply=%region_37.40 | all-reduce | flops 231 | bytes 1848 | tf_op jit(solution)/shard_map/psum | solution.py:79
  1106.3 19.7 %custom-call.50 = f32[2,128,128]{1,2,0:T(8,128)S(1)} custom-call(f32[2,128,128]{2,1,0:T(8,128)S(1)} %pad_maximum_fusion.19), custom_call_target="InvertDiagBlocksLowerTriangular" | custom-call | tf_op jit(solution)/shard_map/jit(_cho_solve)/triangular_solve | solution.py:80
  1127.7 19.1 %psum.118 = f32[231]{0:T(256)S(1)} all-reduce(f32[231]{0:T(256)S(1)} %bitcast.1083), channel_id=1, replica_groups=mesh['book'=4,'path'=8] {'path'}, use_global_device_ids=true, to_apply=%region_40.43 | all-reduce | flops 231 | bytes 1848 | tf_op jit(solution)/shard_map/psum | solution.py:79
  1152.7 17.8 %psum.119 = f32[]{:T(128)} all-reduce(f32[]{:T(128)} %get-tuple-element.84), channel_id=1, replica_groups=mesh['book'=4,'path'=8] {'path'}, use_global_device_ids=true, to_apply=%region_42.45 | all-reduce | flops 1 | bytes 8 | tf_op jit(solution)/shard_map/psum | solution.py:90
  (578 shorter events, 369.9 us)
Async XLA Ops:
  7.2 43.1 %copy-start.113 = (s32[210]{0:T(256)S(1)}, s32[210]{0:T(256)}, u32[]{:S(2)}) copy-start(s32[210]{0:T(256)} %constant.243) | copy-start | bytes 2524
  7.2 43.1 %copy-start.114 = (s32[210]{0:T(256)S(1)}, s32[210]{0:T(256)}, u32[]{:S(2)}) copy-start(s32[210]{0:T(256)} %constant.242) | copy-start | bytes 2524
  7.2 257.9 %all-reduce.6.cloned.1.call-start = ((), (), s32[]{:S(2)}) async-start(), calls=%async_computation | async-start | bytes 4751360 | tf_op jit(solution)/shard_map/psum | solution.py:61
  9.3 123.2 %copy-start.72 = (f32[1,2048]{1,0:T(1,128)}, f32[1,2048]{1,0:T(1,128)S(1)}, u32[]{:S(2)}) copy-start(f32[1,2048]{1,0:T(1,128)S(1)} %get-tuple-element.141) | copy-start | bytes 24580
  9.3 125.9 %copy-start.74 = (f32[1,2048]{1,0:T(1,128)}, f32[1,2048]{1,0:T(1,128)S(1)}, u32[]{:S(2)}) copy-start(f32[1,2048]{1,0:T(1,128)S(1)} %get-tuple-element.140) | copy-start | bytes 24580
  9.3 128.6 %copy-start.76 = (f32[1,2048]{1,0:T(1,128)}, f32[1,2048]{1,0:T(1,128)S(1)}, u32[]{:S(2)}) copy-start(f32[1,2048]{1,0:T(1,128)S(1)} %get-tuple-element.139) | copy-start | bytes 24580
  9.3 131.5 %copy-start.78 = (f32[1,2048]{1,0:T(1,128)}, f32[1,2048]{1,0:T(1,128)S(1)}, u32[]{:S(2)}) copy-start(f32[1,2048]{1,0:T(1,128)S(1)} %get-tuple-element.138) | copy-start | bytes 24580
  9.3 134.2 %copy-start.80 = (f32[1,2048]{1,0:T(1,128)}, f32[1,2048]{1,0:T(1,128)S(1)}, u32[]{:S(2)}) copy-start(f32[1,2048]{1,0:T(1,128)S(1)} %get-tuple-element.137) | copy-start | bytes 24580
  9.3 136.9 %copy-start.83 = (f32[1,2048]{1,0:T(1,128)}, f32[1,2048]{1,0:T(1,128)S(1)}, u32[]{:S(2)}) copy-start(f32[1,2048]{1,0:T(1,128)S(1)} %get-tuple-element.136) | copy-start | bytes 24580
  9.3 139.6 %copy-start.84 = (f32[1,2048]{1,0:T(1,128)}, f32[1,2048]{1,0:T(1,128)S(1)}, u32[]{:S(2)}) copy-start(f32[1,2048]{1,0:T(1,128)S(1)} %get-tuple-element.135) | copy-start | bytes 24580
  9.3 142.3 %copy-start.86 = (f32[1,2048]{1,0:T(1,128)}, f32[1,2048]{1,0:T(1,128)S(1)}, u32[]{:S(2)}) copy-start(f32[1,2048]{1,0:T(1,128)S(1)} %get-tuple-element.134) | copy-start | bytes 24580
  9.3 145.4 %copy-start.89 = (f32[1,2048]{1,0:T(1,128)}, f32[1,2048]{1,0:T(1,128)S(1)}, u32[]{:S(2)}) copy-start(f32[1,2048]{1,0:T(1,128)S(1)} %get-tuple-element.143) | copy-start | bytes 24580
  169.5 133.3 %copy-start.53 = (f32[128,25]{1,0:T(8,128)}, f32[128,25]{1,0:T(8,128)S(1)}, u32[]{:S(2)}) copy-start(f32[128,25]{1,0:T(8,128)S(1)} %pad_convert_fusion) | copy-start | bytes 38404
  172.0 94.8 %copy-start.92 = (f32[2048]{0:T(1024)}, f32[2048]{0:T(1024)S(1)}, u32[]{:S(2)}) copy-start(f32[2048]{0:T(1024)S(1)} %mul.566) | copy-start | bytes 24580
  662.2 53.8 %copy-start.47 = (s32[2048]{0:T(1024)S(1)}, s32[2048]{0:T(1024)}, u32[]{:S(2)}) copy-start(s32[2048]{0:T(1024)} %param.54) | copy-start | bytes 24580
  667.2 49.6 %copy-start.36 = (f32[210,2048]{1,0:T(8,128)S(1)}, f32[210,2048]{1,0:T(8,128)}, u32[]{:S(2)}) copy-start(f32[210,2048]{1,0:T(8,128)} %copy-done.35) | copy-start | bytes 5160964
  742.4 55.2 %copy-start.34 = (f32[210,2048]{1,0:T(8,128)S(1)}, f32[210,2048]{1,0:T(8,128)}, u32[]{:S(2)}) copy-start(f32[210,2048]{1,0:T(8,128)} %copy-done.33) | copy-start | bytes 5160964
  800.6 47.2 %copy-start.32 = (f32[210,2048]{1,0:T(8,128)S(1)}, f32[210,2048]{1,0:T(8,128)}, u32[]{:S(2)}) copy-start(f32[210,2048]{1,0:T(8,128)} %copy-done.31) | copy-start | bytes 5160964
  850.2 46.4 %copy-start.30 = (f32[210,2048]{1,0:T(8,128)S(1)}, f32[210,2048]{1,0:T(8,128)}, u32[]{:S(2)}) copy-start(f32[210,2048]{1,0:T(8,128)} %copy-done.29) | copy-start | bytes 5160964
  876.1 43.8 %copy-start.109 = (f32[1,2048]{1,0:T(1,128)S(1)}, f32[1,2048]{1,0:T(1,128)}, u32[]{:S(2)}) copy-start(f32[1,2048]{1,0:T(1,128)} %copy-done.107) | copy-start | bytes 24580
  899.0 43.2 %copy-start.81 = (f32[1,2048]{1,0:T(1,128)S(1)}, f32[1,2048]{1,0:T(1,128)}, u32[]{:S(2)}) copy-start(f32[1,2048]{1,0:T(1,128)} %copy-done.80) | copy-start | bytes 24580
  899.0 43.2 %copy-start.91 = (f32[2048]{0:T(1024)S(1)}, f32[2048]{0:T(1024)}, u32[]{:S(2)}) copy-start(f32[2048]{0:T(1024)} %reduce_sum.133) | copy-start | bytes 24580
  899.1 43.2 %copy-start.101 = (f32[1,2048]{1,0:T(1,128)S(1)}, f32[1,2048]{1,0:T(1,128)}, u32[]{:S(2)}) copy-start(f32[1,2048]{1,0:T(1,128)} %get-tuple-element.123) | copy-start | bytes 24580
  899.1 43.2 %copy-start.102 = (f32[1,2048]{1,0:T(1,128)S(1)}, f32[1,2048]{1,0:T(1,128)}, u32[]{:S(2)}) copy-start(f32[1,2048]{1,0:T(1,128)} %get-tuple-element.124) | copy-start | bytes 24580
  899.1 43.3 %copy-start.28 = (f32[210,2048]{1,0:T(8,128)S(1)}, f32[210,2048]{1,0:T(8,128)}, u32[]{:S(2)}) copy-start(f32[210,2048]{1,0:T(8,128)} %copy-done.27) | copy-start | bytes 5160964
  899.1 43.3 %copy-start.79 = (f32[1,2048]{1,0:T(1,128)S(1)}, f32[1,2048]{1,0:T(1,128)}, u32[]{:S(2)}) copy-start(f32[1,2048]{1,0:T(1,128)} %copy-done.78) | copy-start | bytes 24580
  944.0 45.0 %copy-start.88 = (f32[2048]{0:T(1024)S(1)}, f32[2048]{0:T(1024)}, u32[]{:S(2)}) copy-start(f32[2048]{0:T(1024)} %reduce_sum.134) | copy-start | bytes 24580
  944.1 45.0 %copy-start.99 = (f32[1,2048]{1,0:T(1,128)S(1)}, f32[1,2048]{1,0:T(1,128)}, u32[]{:S(2)}) copy-start(f32[1,2048]{1,0:T(1,128)} %get-tuple-element.121) | copy-start | bytes 24580
  944.1 45.0 %copy-start.100 = (f32[1,2048]{1,0:T(1,128)S(1)}, f32[1,2048]{1,0:T(1,128)}, u32[]{:S(2)}) copy-start(f32[1,2048]{1,0:T(1,128)} %get-tuple-element.122) | copy-start | bytes 24580
  944.1 45.0 %copy-start.26 = (f32[210,2048]{1,0:T(8,128)S(1)}, f32[210,2048]{1,0:T(8,128)}, u32[]{:S(2)}) copy-start(f32[210,2048]{1,0:T(8,128)} %copy-done.25) | copy-start | bytes 5160964
  944.1 45.0 %copy-start.77 = (f32[1,2048]{1,0:T(1,128)S(1)}, f32[1,2048]{1,0:T(1,128)}, u32[]{:S(2)}) copy-start(f32[1,2048]{1,0:T(1,128)} %copy-done.76) | copy-start | bytes 24580
  990.8 43.3 %copy-start.87 = (f32[2048]{0:T(1024)S(1)}, f32[2048]{0:T(1024)}, u32[]{:S(2)}) copy-start(f32[2048]{0:T(1024)} %reduce_sum.135) | copy-start | bytes 24580
  990.8 43.3 %copy-start.97 = (f32[1,2048]{1,0:T(1,128)S(1)}, f32[1,2048]{1,0:T(1,128)}, u32[]{:S(2)}) copy-start(f32[1,2048]{1,0:T(1,128)} %get-tuple-element.119) | copy-start | bytes 24580
  990.8 43.3 %copy-start.98 = (f32[1,2048]{1,0:T(1,128)S(1)}, f32[1,2048]{1,0:T(1,128)}, u32[]{:S(2)}) copy-start(f32[1,2048]{1,0:T(1,128)} %get-tuple-element.120) | copy-start | bytes 24580
  990.8 43.4 %copy-start.24 = (f32[210,2048]{1,0:T(8,128)S(1)}, f32[210,2048]{1,0:T(8,128)}, u32[]{:S(2)}) copy-start(f32[210,2048]{1,0:T(8,128)} %copy-done.23) | copy-start | bytes 5160964
  990.8 43.4 %copy-start.75 = (f32[1,2048]{1,0:T(1,128)S(1)}, f32[1,2048]{1,0:T(1,128)}, u32[]{:S(2)}) copy-start(f32[1,2048]{1,0:T(1,128)} %copy-done.74) | copy-start | bytes 24580
  1035.9 45.0 %copy-start.85 = (f32[2048]{0:T(1024)S(1)}, f32[2048]{0:T(1024)}, u32[]{:S(2)}) copy-start(f32[2048]{0:T(1024)} %reduce_sum.136) | copy-start | bytes 24580
  1035.9 45.0 %copy-start.95 = (f32[1,2048]{1,0:T(1,128)S(1)}, f32[1,2048]{1,0:T(1,128)}, u32[]{:S(2)}) copy-start(f32[1,2048]{1,0:T(1,128)} %get-tuple-element.117) | copy-start | bytes 24580
  1035.9 45.0 %copy-start.96 = (f32[1,2048]{1,0:T(1,128)S(1)}, f32[1,2048]{1,0:T(1,128)}, u32[]{:S(2)}) copy-start(f32[1,2048]{1,0:T(1,128)} %get-tuple-element.118) | copy-start | bytes 24580
  1035.9 45.0 %copy-start.22 = (f32[210,2048]{1,0:T(8,128)S(1)}, f32[210,2048]{1,0:T(8,128)}, u32[]{:S(2)}) copy-start(f32[210,2048]{1,0:T(8,128)} %copy-done.21) | copy-start | bytes 5160964
  1035.9 45.0 %copy-start.73 = (f32[1,2048]{1,0:T(1,128)S(1)}, f32[1,2048]{1,0:T(1,128)}, u32[]{:S(2)}) copy-start(f32[1,2048]{1,0:T(1,128)} %copy-done.72) | copy-start | bytes 24580
  1082.7 43.3 %copy-start.82 = (f32[2048]{0:T(1024)S(1)}, f32[2048]{0:T(1024)}, u32[]{:S(2)}) copy-start(f32[2048]{0:T(1024)} %reduce_sum.137) | copy-start | bytes 24580
  1082.7 43.3 %copy-start.93 = (f32[1,2048]{1,0:T(1,128)S(1)}, f32[1,2048]{1,0:T(1,128)}, u32[]{:S(2)}) copy-start(f32[1,2048]{1,0:T(1,128)} %get-tuple-element.115) | copy-start | bytes 24580
  1082.7 43.3 %copy-start.94 = (f32[1,2048]{1,0:T(1,128)S(1)}, f32[1,2048]{1,0:T(1,128)}, u32[]{:S(2)}) copy-start(f32[1,2048]{1,0:T(1,128)} %get-tuple-element.116) | copy-start | bytes 24580
  1082.7 43.3 %copy-start.20 = (f32[210,2048]{1,0:T(8,128)S(1)}, f32[210,2048]{1,0:T(8,128)}, u32[]{:S(2)}) copy-start(f32[210,2048]{1,0:T(8,128)} %copy-done.19) | copy-start | bytes 5160964
  1127.7 43.4 %copy-start.110 = (f32[1,231]{1,0:T(1,128)S(1)}, f32[1,231]{1,0:T(1,128)}, u32[]{:S(2)}) copy-start(f32[1,231]{1,0:T(1,128)} %fusion.420) | copy-start | bytes 2776
  1127.7 43.4 %copy-start.111 = (f32[1,231]{1,0:T(1,128)S(1)}, f32[1,231]{1,0:T(1,128)}, u32[]{:S(2)}) copy-start(f32[1,231]{1,0:T(1,128)} %fusion.419) | copy-start | bytes 2776
  1127.7 43.4 %copy-start.112 = (f32[1,231]{1,0:T(1,128)S(1)}, f32[1,231]{1,0:T(1,128)}, u32[]{:S(2)}) copy-start(f32[1,231]{1,0:T(1,128)} %fusion.418) | copy-start | bytes 2776
  (68 other events, 730.7 us)
Sparse Core Ops, SparseCore 0:
  157.6 107.4 all-reduce.5
where the time goes:
time: 1190 us; the launch traced here: 1180 us
  other arithmetic  612 us (51%)
  blocking collectives  241 us (20%)
  matrix products  126 us (11%)
  local copies, waits for them, and re-layouts  102 us (9%)
  waiting for transfers between devices  67.7 us (6%)
  between operations  31.7 us (3%)
    another operation x70, other arithmetic, shards(): jnp.linalg.cholesky(system_of(gram_stack[date_step], count_all[date_step]))  342 us
    another operation x34, other arithmetic, shards(): jax.scipy.linalg.cho_solve((chol_list[date_step], True), rhs_total / coun...  212 us
    psum x10, blocking collectives, shards(): rhs_total = lax.psum(rhs_local, 'path')  185 us
    psum x1, waiting for transfers between devices, shards(): gram_stack = lax.psum(jnp.stack(local_list, axis=0), 'path')  67.7 us
    psum x1, blocking collectives, shards(): lax.psum((jnp.sum(money_all, axis=1), jnp.sum(money_all[:, None, :] * sta...  38.8 us
    another operation x60, matrix products, shards(): jax.scipy.linalg.cho_solve((chol_list[date_step], True), rhs_total / coun...  28.7 us
    dot_general x10, matrix products, gram_only(): lax.dot_general(weighted, basis_rows, (((1,), (1,)), ((), ())), precision...  27.7 us
    dot_general x10, matrix products, shards(): jnp.dot(coef_vector, basis_rows, precision=highest, preferred_element_typ...  27.6 us
  transfers between devices with their start and end apart: 1, of which 1 were waited for; matrix products, arithmetic and copies ran while one was open for 2% of the time, Pallas kernels for 0%

commit v1 on v0

v1 whole, which is shorter than its diff:
```python
import functools

import jax
import jax.numpy as jnp
from jax import lax
from jax.experimental import pallas as pl
from jax.experimental.pallas import tpu as pltpu
from jax.sharding import PartitionSpec as P

ridge_weight = 0.05
temper_scale = 0.5
highest = lax.Precision.HIGHEST
LANES = 128
BLOCK = 32
MESH = pl.DeviceIdType.MESH
VM = pl.BlockSpec(memory_space=pltpu.VMEM)


def round_up(n, k):
    return -(-n // k) * k


def peer(me, offset, n):
    return lax.rem(me + offset, n)


def entry_barrier(me, n):
    barrier = pltpu.get_barrier_semaphore()
    for o in range(1, n):
        pl.semaphore_signal(barrier, inc=1, device_id={"path": peer(me, o, n)}, device_id_type=MESH)
    pl.semaphore_wait(barrier, n - 1)


def column(stats, d):
    lane = lax.broadcasted_iota(jnp.int32, stats.shape, 1)
    return jnp.sum(jnp.where(lane == d, stats, 0.0), axis=1, keepdims=True)


def build_basis(z, mean, inv_scale, store):
    n = z.shape[0]
    x = (z - mean) * inv_scale
    store(0, jnp.ones((1, z.shape[1]), jnp.float32))
    store(1, x)
    at = 1 + n
    for j in range(n):
        store(at, x[j:j + 1] * x[j:])
        at += n - j
    return at


def stats_kernel(n, states, flags, out, mine, got, send_sem, recv_sem):
    me = lax.axis_index("path")
    dates, factors, _ = states.shape
    rows = round_up(factors, 8)
    lane = lax.broadcasted_iota(jnp.int32, (1, LANES), 1)
    first = jnp.zeros((factors, LANES), jnp.float32)
    second = jnp.zeros((factors, LANES), jnp.float32)
    count = jnp.zeros((1, LANES), jnp.float32)
    for d in range(dates):
        m = flags[d:d + 1, :].astype(jnp.float32)
        z = states[d]
        mz = m * z
        first = jnp.where(lane == d, jnp.sum(mz, axis=1, keepdims=True), first)
        second = jnp.where(lane == d, jnp.sum(mz * z, axis=1, keepdims=True), second)
        count = jnp.where(lane == d, jnp.sum(m, axis=1, keepdims=True), count)
    mine[...] = jnp.zeros_like(mine)
    mine[0:factors, :] = first
    mine[rows:rows + factors, :] = second
    mine[2 * rows:2 * rows + 1, :] = count
    entry_barrier(me, n)

    def copy(o):
        return pltpu.make_async_remote_copy(
            src_ref=mine, dst_ref=got.at[me], send_sem=send_sem.at[o], recv_sem=recv_sem.at[me],
            device_id={"path": peer(me, o, n)}, device_id_type=MESH)

    for o in range(1, n):
        copy(o).start()
    got[me] = mine[...]
    for o in range(1, n):
        p = peer(me, o, n)
        pltpu.make_async_remote_copy(
            src_ref=mine, dst_ref=got.at[p], send_sem=send_sem.at[o], recv_sem=recv_sem.at[p],
            device_id={"path": p}, device_id_type=MESH).wait_recv()
    total = got[0]
    for p in range(1, n):
        total = total + got[p]
    live = lane < dates
    count = jnp.where(live, total[2 * rows:2 * rows + 1], 1.0)
    mean = total[0:rows] / count
    variance = total[rows:2 * rows] / count - mean * mean
    scale = jnp.sqrt(jnp.where(live, variance, 0.0) + 1e-05)
    out[0:rows, :] = mean
    out[rows:2 * rows, :] = 1.0 / scale
    out[2 * rows:2 * rows + 8, :] = jnp.broadcast_to(count, (8, LANES))
    for o in range(1, n):
        copy(o).wait_send()


def gram_kernel(states, flags, stats, out, phi):
    d = pl.program_id(0)
    z = states[0]
    factors = z.shape[0]
    rows = round_up(factors, 8)
    m = flags[0].astype(jnp.float32)
    mean = column(stats[0:rows, :], d)[0:factors]
    inv_scale = column(stats[rows:2 * rows, :], d)[0:factors]
    size = phi.shape[0]

    def store(at, value):
        phi[at:at + value.shape[0], :] = value * m

    used = build_basis(z, mean, inv_scale, store)
    if used < size:
        phi[used:size, :] = jnp.zeros((size - used, z.shape[1]), jnp.float32)
    w = phi[...]
    hi = w.astype(jnp.bfloat16)
    rest = w - hi.astype(jnp.float32)
    mid = rest.astype(jnp.bfloat16)
    low = (rest - mid.astype(jnp.float32)).astype(jnp.bfloat16)

    def nt(a, b):
        return lax.dot_general(a, b, (((1,), (1,)), ((), ())), preferred_element_type=jnp.float32)

    cross = nt(hi, mid) + nt(hi, low)
    out[0] = (nt(hi, hi) + nt(mid, mid)) + (cross + cross.T)


def reduce_kernel(n, basis, grams, stats, out, got, send_sem, recv_sem):
    me = lax.axis_index("path")
    dates, size, _ = grams.shape
    slots = out.shape[0]
    count_row = stats.shape[0] - 8
    entry_barrier(me, n)

    def copy(e):
        owner, slot = e % n, e // n
        return pltpu.make_async_remote_copy(
            src_ref=grams.at[e], dst_ref=got.at[me, slot], send_sem=send_sem.at[e],
            recv_sem=recv_sem.at[me, slot], device_id={"path": owner}, device_id_type=MESH)

    for e in range(dates):
        @pl.when(me != e % n)
        def _():
            copy(e).start()
    ri = lax.broadcasted_iota(jnp.int32, (size, size), 0)
    ci = lax.broadcasted_iota(jnp.int32, (size, size), 1)
    for slot in range(slots):
        e = me + slot * n

        @pl.when(e < dates)
        def _():
            for o in range(1, n):
                p = peer(me, o, n)
                pltpu.make_async_remote_copy(
                    src_ref=grams.at[0], dst_ref=got.at[p, slot], send_sem=send_sem.at[0],
                    recv_sem=recv_sem.at[p, slot], device_id={"path": p}, device_id_type=MESH).wait_recv()
            total = grams[e]
            for o in range(1, n):
                total = total + got[peer(me, o, n), slot]
            count = column(stats[count_row:count_row + 8, :], e)[0:1]
            diag = jnp.where(ri < basis, ridge_weight, 1.0)
            out[slot] = total / count + jnp.where(ri == ci, diag, 0.0)

        @pl.when(e >= dates)
        def _():
            out[slot] = jnp.where(ri == ci, 1.0, 0.0)
    for e in range(dates):
        @pl.when(me != e % n)
        def _():
            copy(e).wait_send()


def small_inverse(d_list):
    b = d_list[0].shape[0]
    sub = lax.broadcasted_iota(jnp.int32, (b, b), 0)
    lane = lax.broadcasted_iota(jnp.int32, (b, b), 1)
    lane_row = lax.broadcasted_iota(jnp.int32, (1, b), 1)
    for j in range(b):
        new = []
        for d in d_list:
            inv = 1.0 / d[j:j + 1, j:j + 1]
            row = jnp.where(lane_row == j, inv, d[j:j + 1, :] * inv)
            col = d[:, j:j + 1]
            new.append(jnp.where(sub == j, row, jnp.where(lane == j, 0.0, d) - col * row))
        d_list = new
    return d_list


def inverse_kernel(system, out, work):
    slots, size, _ = system.shape
    work[...] = system[...]
    for k in range(size // BLOCK):
        lo, hi = k * BLOCK, (k + 1) * BLOCK
        diag = small_inverse([work[s, lo:hi, lo:hi] for s in range(slots)])
        for s in range(slots):
            rows = work[s, lo:hi, :]
            r = jnp.dot(diag[s], rows, precision=highest, preferred_element_type=jnp.float32)
            update = lax.dot_general(rows, r, (((0,), (0,)), ((), ())), precision=highest,
                                     preferred_element_type=jnp.float32)
            work[s] = work[s] - update
            work[s, lo:hi, :] = r
            work[s, :, lo:hi] = r.T
            work[s, lo:hi, lo:hi] = -diag[s]
    out[...] = -work[...]


def backward_kernel(n, states, flags, terminal, strike, date_index, stats, inverse,
                    flow, price, coefs,
                    phi, terms, inv_all, rhs_mine, rhs_got, sum_mine, sum_got,
                    inv_send, inv_recv, rhs_send, rhs_recv, sum_send, sum_recv):
    me = lax.axis_index("path")
    dates, factors, paths = states.shape
    size = phi.shape[1]
    rows = round_up(factors, 8)
    tiles = paths // LANES
    entry_barrier(me, n)

    def inv_copy(e, o):
        return pltpu.make_async_remote_copy(
            src_ref=inverse.at[e // n], dst_ref=inv_all.at[e], send_sem=inv_send.at[e, o],
            recv_sem=inv_recv.at[e], device_id={"path": peer(me, o, n)}, device_id_type=MESH)

    def own_copy(e):
        return pltpu.make_async_copy(inverse.at[e // n], inv_all.at[e], inv_recv.at[e])

    for e in range(dates - 1, -1, -1):
        @pl.when(me == e % n)
        def _():
            for o in range(1, n):
                inv_copy(e, o).start()
            own_copy(e).start()

    def prepare(d, slot):
        z = states[d]
        mean = column(stats[0:rows, :], d)[0:factors]
        inv_scale = column(stats[rows:2 * rows, :], d)[0:factors]

        def store(at, value):
            phi[slot, at:at + value.shape[0], :] = value

        used = build_basis(z, mean, inv_scale, store)
        if used < size:
            phi[slot, used:size, :] = jnp.zeros((size - used, paths), jnp.float32)
        step = 1.0 / (1.0 + 0.25 * (0.03 * jnp.exp(0.25 * z)))
        discount = step[0:1]
        total = discount
        for j in range(1, factors):
            discount = discount * step[j:j + 1]
            total = total + discount
        annuity = 0.25 * total
        swap_rate = (1.0 - discount) / annuity
        terms[slot, 0:1, :] = 100.0 * annuity * (swap_rate - strike[...])
        terms[slot, 1:2, :] = step[0:1]

    prepare(dates - 1, 0)
    coefs[...] = jnp.zeros_like(coefs)
    lane = lax.broadcasted_iota(jnp.int32, (1, LANES), 1)
    flow[...] = terminal[...]

    def rhs_copy(d, o):
        return pltpu.make_async_remote_copy(
            src_ref=rhs_mine.at[d], dst_ref=rhs_got.at[d, me], send_sem=rhs_send.at[d, o],
            recv_sem=rhs_recv.at[d, me], device_id={"path": peer(me, o, n)}, device_id_type=MESH)

    def step(i, carry):
        d = dates - 1 - i
        slot = lax.rem(i, 2)
        money = flags[pl.ds(d, 1), :].astype(jnp.float32)
        exercise = terms[slot, 0:1, :]
        value = flow[...] * terms[slot, 1:2, :]
        masked = value * money
        acc = jnp.zeros((size, LANES), jnp.float32)
        for t in range(tiles):
            cols = slice(t * LANES, (t + 1) * LANES)
            acc = acc + phi[slot, :, cols] * masked[:, cols]
        part = jnp.sum(acc.T.reshape(LANES // 8, 8, size), axis=0)
        rhs_mine[d] = part
        for o in range(1, n):
            rhs_copy(d, o).start()
        rhs_got[d, me] = part
        prepare(lax.max(d - 1, 0), 1 - slot)
        pltpu.make_async_copy(inverse.at[0], inv_all.at[d], inv_recv.at[d]).wait()
        for o in range(1, n):
            p = peer(me, o, n)
            pltpu.make_async_remote_copy(
                src_ref=rhs_mine.at[d], dst_ref=rhs_got.at[d, p], send_sem=rhs_send.at[d, o],
                recv_sem=rhs_recv.at[d, p], device_id={"path": p}, device_id_type=MESH).wait_recv()
        total = rhs_got[d, 0]
        for p in range(1, n):
            total = total + rhs_got[d, p]
        count = column(stats[2 * rows:2 * rows + 8, :], d)[0:1]
        rhs = jnp.sum(total, axis=0, keepdims=True) / count
        coef = jnp.sum(inv_all[d] * rhs, axis=1, keepdims=True)
        coefs[...] = jnp.where(lane == d, coef, coefs[...])
        coef_wide = jnp.broadcast_to(coef, (size, LANES))
        parts = []
        for t in range(tiles):
            cols = slice(t * LANES, (t + 1) * LANES)
            parts.append(jnp.sum(phi[slot, :, cols] * coef_wide, axis=0, keepdims=True))
        continuation = jnp.concatenate(parts, axis=1)
        open_date = jnp.where(date_index[...] <= d, money, 0.0)
        weights = jax.nn.sigmoid((exercise - continuation) / temper_scale) * open_date
        flow[...] = value + weights * (exercise - value)
        for o in range(1, n):
            rhs_copy(d, o).wait_send()
        return carry

    lax.fori_loop(0, dates, step, 0)

    final = flow[...]
    part = final[:, 0:LANES]
    for t in range(1, tiles):
        part = part + final[:, t * LANES:(t + 1) * LANES]
    wide = jnp.broadcast_to(part, (8, LANES))
    sum_mine[...] = wide

    def sum_copy(o):
        return pltpu.make_async_remote_copy(
            src_ref=sum_mine, dst_ref=sum_got.at[me], send_sem=sum_send.at[o],
            recv_sem=sum_recv.at[me], device_id={"path": peer(me, o, n)}, device_id_type=MESH)

    for o in range(1, n):
        sum_copy(o).start()
    sum_got[me] = wide
    for o in range(1, n):
        p = peer(me, o, n)
        pltpu.make_async_remote_copy(
            src_ref=sum_mine, dst_ref=sum_got.at[p], send_sem=sum_send.at[o],
            recv_sem=sum_recv.at[p], device_id={"path": p}, device_id_type=MESH).wait_recv()
    total = sum_got[0]
    for p in range(1, n):
        total = total + sum_got[p]
    price[...] = jnp.sum(total[0:1], axis=1, keepdims=True) / (paths * n)
    for o in range(1, n):
        sum_copy(o).wait_send()
    for e in range(dates):
        @pl.when(me == e % n)
        def _():
            for o in range(1, n):
                inv_copy(e, o).wait_send()


def shards(states, itm_flags, terminal, strike, date_index):
    n = lax.axis_size("path")
    dates, factors, paths = states.shape
    f32 = jnp.float32
    basis = 1 + factors + factors * (factors + 1) // 2
    size = round_up(basis, LANES)
    slots = -(-dates // n)
    rows = round_up(factors, 8)
    dma = pltpu.SemaphoreType.DMA
    big = 60 << 20

    def params(cid):
        return pltpu.CompilerParams(collective_id=cid, has_side_effects=True, vmem_limit_bytes=big)

    stats = pl.pallas_call(
        functools.partial(stats_kernel, n),
        out_shape=jax.ShapeDtypeStruct((2 * rows + 8, LANES), f32),
        in_specs=[VM, VM], out_specs=VM,
        scratch_shapes=[pltpu.VMEM((2 * rows + 8, LANES), f32),
                        pltpu.VMEM((n, 2 * rows + 8, LANES), f32), dma((n,)), dma((n,))],
        compiler_params=params(0), name="stats")(states, itm_flags)

    grams = pl.pallas_call(
        gram_kernel, grid=(dates,),
        out_shape=jax.ShapeDtypeStruct((dates, size, size), f32),
        in_specs=[pl.BlockSpec((1, factors, paths), lambda d: (d, 0, 0)),
                  pl.BlockSpec((1, 1, paths), lambda d: (d, 0, 0)),
                  VM],
        out_specs=pl.BlockSpec((1, size, size), lambda d: (d, 0, 0)),
        scratch_shapes=[pltpu.VMEM((size, paths), f32)],
        compiler_params=pltpu.CompilerParams(vmem_limit_bytes=big), name="gram",
    )(states, itm_flags[:, None, :], stats)

    system = pl.pallas_call(
        functools.partial(reduce_kernel, n, basis),
        out_shape=jax.ShapeDtypeStruct((slots, size, size), f32),
        in_specs=[VM, VM], out_specs=VM,
        scratch_shapes=[pltpu.VMEM((n, slots, size, size), f32), dma((dates,)), dma((n, slots))],
        compiler_params=params(1), name="reduce")(grams, stats)

    inverse = pl.pallas_call(
        inverse_kernel,
        out_shape=jax.ShapeDtypeStruct((slots, size, size), f32),
        in_specs=[VM], out_specs=VM,
        scratch_shapes=[pltpu.VMEM((slots, size, size), f32)],
        compiler_params=pltpu.CompilerParams(vmem_limit_bytes=big), name="inverse")(system)

    flow, price, coefs = pl.pallas_call(
        functools.partial(backward_kernel, n),
        out_shape=(jax.ShapeDtypeStruct((1, paths), f32), jax.ShapeDtypeStruct((1, 1), f32),
                   jax.ShapeDtypeStruct((size, LANES), f32)),
        in_specs=[VM] * 7, out_specs=(VM, VM, VM),
        scratch_shapes=[pltpu.VMEM((2, size, paths), f32), pltpu.VMEM((2, 8, paths), f32),
                        pltpu.VMEM((dates, size, size), f32),
                        pltpu.VMEM((dates, 8, size), f32), pltpu.VMEM((dates, n, 8, size), f32),
                        pltpu.VMEM((8, LANES), f32), pltpu.VMEM((n, 8, LANES), f32),
                        dma((dates, n)), dma((dates,)), dma((dates, n)), dma((dates, n)),
                        dma((n,)), dma((n,))],
        compiler_params=params(2), name="backward",
    )(states, itm_flags, terminal.reshape(1, paths), strike.reshape(1, 1),
      date_index.reshape(1, paths), stats, inverse)
    return flow.reshape(paths), price.reshape(1), coefs[:basis, :dates].T


def solution(mesh):
    in_specs = (
        P(None, None, ("book", "path")),
        P(None, ("book", "path")),
        P(("book", "path")),
        P("book"),
        P(("book", "path")),
    )
    out_specs = (P(("book", "path")), P("book"), P("book", None))
    return jax.shard_map(shards, mesh=mesh, in_specs=in_specs, out_specs=out_specs, check_vma=False)
```

time: 1190 us -> 274 us (0.23)
  other arithmetic: 612 us -> 0 us
  Pallas kernels: 0 us -> 266 us
  blocking collectives: 241 us -> 0 us
  matrix products: 126 us -> 0 us
  local copies, waits for them, and re-layouts: 102 us -> 4.48 us
  waiting for transfers between devices: 67.7 us -> 0 us
  between operations: 31.7 us -> 3.07 us
    another operation x124 -> x0, other arithmetic: 560 us -> none  [the longest x70 342 us: shards(): jnp.linalg.cholesky(system_of(gram_stack[date_step], count_all[date_step]))]
    pallas_call x0 -> x5, Pallas kernels: none -> 266 us  [the longest x1 130 us: shards(): pl.pallas_call(functools.partial(backward_kernel, n), out_shape=(jax.Shap...]
    psum x12 -> x0, blocking collectives: 241 us -> none  [the longest x10 185 us: shards(): rhs_total = lax.psum(rhs_local, 'path')]
    dot_general x30 -> x0, matrix products: 77.4 us -> none  [the longest x10 27.7 us: gram_only(): lax.dot_general(weighted, basis_rows, (((1,), (1,)), ((), ())), precision...]
    psum x1 -> x0, waiting for transfers between devices: 67.7 us -> none  [shards(): gram_stack = lax.psum(jnp.stack(local_list, axis=0), 'path')]
    gather x20 -> x0, local copies, waits for them, and re-layouts: 49.4 us -> none  [the longest x10 25 us: basis_of(): scaled[pair_left] * scaled[pair_right]]
    another operation x80 -> x0, matrix products: 48.2 us -> none  [the longest x60 28.7 us: shards(): jax.scipy.linalg.cho_solve((chol_list[date_step], True), rhs_total / coun...]
    unnamed x230 -> x2, local copies, waits for them, and re-layouts: 24.9 us -> 1.98 us
  transfers between devices with their start and end apart: 1 -> 0, of which waited for: 1 -> 0; matrix products, arithmetic and copies ran while one was open for 2% -> 0% of each run, Pallas kernels for 0% -> 0%
where the time goes in v1:
time: 274 us
  Pallas kernels  266 us (97%)
  local copies, waits for them, and re-layouts  4.48 us (2%)
  between operations  3.07 us (1%)
    pallas_call x1, Pallas kernels, shards(): pl.pallas_call(functools.partial(backward_kernel, n), out_shape=(jax.Shap...  130 us
    pallas_call x1, Pallas kernels, shards(): pl.pallas_call(functools.partial(reduce_kernel, n, basis), out_shape=jax....  71.3 us
    pallas_call x1, Pallas kernels, shards(): pl.pallas_call(inverse_kernel, out_shape=jax.ShapeDtypeStruct((slots, siz...  30.5 us
    pallas_call x1, Pallas kernels, shards(): pl.pallas_call(gram_kernel, grid=(dates,), out_shape=jax.ShapeDtypeStruct...  21.5 us
    pallas_call x1, Pallas kernels, shards(): pl.pallas_call(functools.partial(stats_kernel, n), out_shape=jax.ShapeDty...  13 us

profile of v1, /device:TPU:0, one launch (start us, length us, event | category | flops | bytes accessed | tf_op | source)
XLA Modules:
  0.0 273.8 jit_solution(7361163338758798157)
XLA Ops:
  0.6 13.0 %stats.1 = f32[56,128]{1,0:T(8,128)} custom-call(f32[10,20,2048]{2,1,0:T(8,128)} %states.5, s32[10,2048]{1,0:T(8,128)} %flags.3), custom_call_target="tpu_custom_call" | custom-call | tf_op jit(solution)/shard_map/stats/pallas_call | solution.py:358
  13.6 1.6 broadcast_in_dim.3.flags
  15.2 21.5 %gram.1.grams = f32[10,256,256]{2,1,0:T(8,128)} custom-call(f32[10,20,2048]{2,1,0:T(8,128)} %states.5, s32[10,1,2048]{2,1,0:T(1,128)} %broadcast_in_dim.3.flags, f32[56,128]{1,0:T(8,128)} %stats.1), custom_call_target="tpu_custom_call" | custom-call | tf_op jit(solution)/shard_map/gram/pallas_call | solution.py:366
  36.7 71.3 %reduce.1.system = f32[2,256,256]{2,1,0:T(8,128)} custom-call(f32[10,256,256]{2,1,0:T(8,128)} %gram.1.grams, f32[56,128]{1,0:T(8,128)} %stats.1), custom_call_target="tpu_custom_call" | custom-call | tf_op jit(solution)/shard_map/reduce/pallas_call | solution.py:377
  108.0 30.5 %inverse.1 = f32[2,256,256]{2,1,0:T(8,128)} custom-call(f32[2,256,256]{2,1,0:T(8,128)} %reduce.1.system), custom_call_target="tpu_custom_call" | custom-call | tf_op jit(solution)/shard_map/inverse/pallas_call | solution.py:384
  139.2 130.0 %backward.1 = (f32[1,2048]{1,0:T(1,128)}, f32[1,1]{1,0:T(1,128)}, f32[256,128]{1,0:T(8,128)}) custom-call(f32[10,20,2048]{2,1,0:T(8,128)} %states.5, s32[10,2048]{1,0:T(8,128)} %flags.3, f32[1,2048]{1,0:T(1,128)} %bitcast.8, f32[1,1]{1,0:T(1,128)} %bitcast.7.strike, s32[1,2048]{1,0:T(1,128)} %bitcast.9, f32[56,128]{1,0:T(8,128)} %stats.1, f32[2,256,256]{2,1,0:T(8,128)} %inverse.1), custom_call_target="tpu_custom_call" | custom-call | tf_op jit(solution)/shard_map/backward/pallas_call | solution.py:391
  269.2 0.9 slice_bitcast_fusion
  270.1 0.7 copy.8
  270.8 1.3 copy.12

commit v2 on v1

--- a/solution.py
+++ b/solution.py
@@ -97,52 +97,66 @@
         copy(o).wait_send()
 
 
-def gram_kernel(states, flags, stats, out, phi):
-    d = pl.program_id(0)
-    z = states[0]
-    factors = z.shape[0]
+def half_iotas():
+    shape = (LANES, LANES)
+    return lax.broadcasted_iota(jnp.int32, shape, 0), lax.broadcasted_iota(jnp.int32, shape, 1)
+
+
+def fold(upper_left, lower_right):
+    ri, ci = half_iotas()
+    return jnp.where(ci <= ri, upper_left, pltpu.roll(lower_right, 1, 1))
+
+
+def unfold(folded):
+    ri, ci = half_iotas()
+    shifted = pltpu.roll(folded, LANES - 1, 1)
+    return (jnp.where(ci <= ri, folded, folded.T), jnp.where(ci >= ri, shifted, shifted.T))
+
+
+def gram_kernel(n, basis, states, flags, stats, out, phi, packed, got, send_sem, recv_sem):
+    me = lax.axis_index("path")
+    dates, factors, paths = states.shape
     rows = round_up(factors, 8)
-    m = flags[0].astype(jnp.float32)
-    mean = column(stats[0:rows, :], d)[0:factors]
-    inv_scale = column(stats[rows:2 * rows, :], d)[0:factors]
     size = phi.shape[0]
-
-    def store(at, value):
-        phi[at:at + value.shape[0], :] = value * m
-
-    used = build_basis(z, mean, inv_scale, store)
-    if used < size:
-        phi[used:size, :] = jnp.zeros((size - used, z.shape[1]), jnp.float32)
-    w = phi[...]
-    hi = w.astype(jnp.bfloat16)
-    rest = w - hi.astype(jnp.float32)
-    mid = rest.astype(jnp.bfloat16)
-    low = (rest - mid.astype(jnp.float32)).astype(jnp.bfloat16)
+    slots = out.shape[0]
+    height = packed.shape[1]
+    entry_barrier(me, n)
+    start = basis // 8 * 8
+    phi[start:size, :] = jnp.zeros((size - start, paths), jnp.float32)
 
     def nt(a, b):
         return lax.dot_general(a, b, (((1,), (1,)), ((), ())), preferred_element_type=jnp.float32)
 
-    cross = nt(hi, mid) + nt(hi, low)
-    out[0] = (nt(hi, hi) + nt(mid, mid)) + (cross + cross.T)
-
-
-def reduce_kernel(n, basis, grams, stats, out, got, send_sem, recv_sem):
-    me = lax.axis_index("path")
-    dates, size, _ = grams.shape
-    slots = out.shape[0]
-    count_row = stats.shape[0] - 8
-    entry_barrier(me, n)
-
     def copy(e):
-        owner, slot = e % n, e // n
         return pltpu.make_async_remote_copy(
-            src_ref=grams.at[e], dst_ref=got.at[me, slot], send_sem=send_sem.at[e],
-            recv_sem=recv_sem.at[me, slot], device_id={"path": owner}, device_id_type=MESH)
-
-    for e in range(dates):
-        @pl.when(me != e % n)
-        def _():
-            copy(e).start()
+            src_ref=packed.at[e], dst_ref=got.at[me, e // n], send_sem=send_sem.at[e],
+            recv_sem=recv_sem.at[me, e // n], device_id={"path": lax.rem(e, n)}, device_id_type=MESH)
+
+    def step(d, carry):
+        m = flags[pl.ds(d, 1), :].astype(jnp.float32)
+        mean = column(stats[0:rows, :], d)[0:factors]
+        inv_scale = column(stats[rows:2 * rows, :], d)[0:factors]
+
+        def store(at, value):
+            phi[at:at + value.shape[0], :] = value * m
+
+        build_basis(states[d], mean, inv_scale, store)
+        w = phi[...]
+        hi = w.astype(jnp.bfloat16)
+        rest = w - hi.astype(jnp.float32)
+        mid = rest.astype(jnp.bfloat16)
+        low = (rest - mid.astype(jnp.float32)).astype(jnp.bfloat16)
+        cross = nt(hi, mid) + nt(hi, low)
+        gram = (nt(hi, hi) + nt(mid, mid)) + (cross + cross.T)
+        packed[d, 0:LANES, :] = fold(gram[0:LANES, 0:LANES], gram[LANES:, LANES:])
+        packed[d, LANES:height, :] = gram[LANES:height, 0:LANES]
+
+        @pl.when(me != lax.rem(d, n))
+        def _():
+            copy(d).start()
+        return carry
+
+    lax.fori_loop(0, dates, step, 0)
     ri = lax.broadcasted_iota(jnp.int32, (size, size), 0)
     ci = lax.broadcasted_iota(jnp.int32, (size, size), 1)
     for slot in range(slots):
@@ -153,14 +167,19 @@
             for o in range(1, n):
                 p = peer(me, o, n)
                 pltpu.make_async_remote_copy(
-                    src_ref=grams.at[0], dst_ref=got.at[p, slot], send_sem=send_sem.at[0],
+                    src_ref=packed.at[0], dst_ref=got.at[p, slot], send_sem=send_sem.at[0],
                     recv_sem=recv_sem.at[p, slot], device_id={"path": p}, device_id_type=MESH).wait_recv()
-            total = grams[e]
+            total = packed[e]
             for o in range(1, n):
                 total = total + got[peer(me, o, n), slot]
-            count = column(stats[count_row:count_row + 8, :], e)[0:1]
-            diag = jnp.where(ri < basis, ridge_weight, 1.0)
-            out[slot] = total / count + jnp.where(ri == ci, diag, 0.0)
+            first, last = unfold(total[0:LANES])
+            below = jnp.concatenate(
+                [total[LANES:], jnp.zeros((size - height, LANES), jnp.float32)], axis=0)
+            full = jnp.concatenate([jnp.concatenate([first, below.T], axis=1),
+                                    jnp.concatenate([below, last], axis=1)], axis=0)
+            count = column(stats[2 * rows:2 * rows + 8, :], e)[0:1]
+            full = jnp.where((ri < basis) & (ci < basis), full / count, 0.0)
+            out[slot] = full + jnp.where(ri == ci, jnp.where(ri < basis, ridge_weight, 1.0), 0.0)
 
         @pl.when(e >= dates)
         def _():
@@ -171,12 +190,12 @@
             copy(e).wait_send()
 
 
-def small_inverse(d_list):
+def small_inverse(d_list, live):
     b = d_list[0].shape[0]
     sub = lax.broadcasted_iota(jnp.int32, (b, b), 0)
     lane = lax.broadcasted_iota(jnp.int32, (b, b), 1)
     lane_row = lax.broadcasted_iota(jnp.int32, (1, b), 1)
-    for j in range(b):
+    for j in range(live):
         new = []
         for d in d_list:
             inv = 1.0 / d[j:j + 1, j:j + 1]
@@ -187,12 +206,13 @@
     return d_list
 
 
-def inverse_kernel(system, out, work):
+def inverse_kernel(basis, system, out, work):
     slots, size, _ = system.shape
     work[...] = system[...]
-    for k in range(size // BLOCK):
+    for k in range(-(-basis // BLOCK)):
         lo, hi = k * BLOCK, (k + 1) * BLOCK
-        diag = small_inverse([work[s, lo:hi, lo:hi] for s in range(slots)])
+        diag = small_inverse([work[s, lo:hi, lo:hi] for s in range(slots)],
+                             min(BLOCK, basis - lo))
         for s in range(slots):
             rows = work[s, lo:hi, :]
             r = jnp.dot(diag[s], rows, precision=highest, preferred_element_type=jnp.float32)
@@ -202,12 +222,15 @@
             work[s, lo:hi, :] = r
             work[s, :, lo:hi] = r.T
             work[s, lo:hi, lo:hi] = -diag[s]
-    out[...] = -work[...]
-
-
-def backward_kernel(n, states, flags, terminal, strike, date_index, stats, inverse,
+    height = out.shape[1]
+    for s in range(slots):
+        out[s, 0:LANES, :] = -fold(work[s, 0:LANES, 0:LANES], work[s, LANES:, LANES:])
+        out[s, LANES:height, :] = -work[s, LANES:height, 0:LANES]
+
+
+def backward_kernel(n, ahead, states, flags, terminal, strike, date_index, stats, inverse,
                     flow, price, coefs,
-                    phi, terms, inv_all, rhs_mine, rhs_got, sum_mine, sum_got,
+                    phi, terms, inv_all, inv_full, rhs_mine, rhs_got, sum_mine, sum_got,
                     inv_send, inv_recv, rhs_send, rhs_recv, sum_send, sum_recv):
     me = lax.axis_index("path")
     dates, factors, paths = states.shape
@@ -224,12 +247,17 @@
     def own_copy(e):
         return pltpu.make_async_copy(inverse.at[e // n], inv_all.at[e], inv_recv.at[e])
 
-    for e in range(dates - 1, -1, -1):
-        @pl.when(me == e % n)
-        def _():
+    def send_inverse(e, live):
+        @pl.when(live & (me == lax.rem(e, n)))
+        def _():
+            own_copy(e).start()
             for o in range(1, n):
                 inv_copy(e, o).start()
-            own_copy(e).start()
+
+    for e in range(dates - 1, dates - 1 - ahead, -1):
+        send_inverse(e, me >= 0)
+    inv_full[...] = jnp.zeros_like(inv_full)
+    height = inv_all.shape[1]
 
     def prepare(d, slot):
         z = states[d]
@@ -279,8 +307,14 @@
         for o in range(1, n):
             rhs_copy(d, o).start()
         rhs_got[d, me] = part
+        send_inverse(lax.max(d - ahead, 0), d >= ahead)
         prepare(lax.max(d - 1, 0), 1 - slot)
         pltpu.make_async_copy(inverse.at[0], inv_all.at[d], inv_recv.at[d]).wait()
+        first, last = unfold(inv_all[d, 0:LANES, :])
+        inv_full[0:LANES, 0:LANES] = first
+        inv_full[LANES:, LANES:] = last
+        inv_full[LANES:height, 0:LANES] = inv_all[d, LANES:height, :]
+        inv_full[0:LANES, LANES:] = inv_full[LANES:, 0:LANES].T
         for o in range(1, n):
             p = peer(me, o, n)
             pltpu.make_async_remote_copy(
@@ -291,7 +325,7 @@
             total = total + rhs_got[d, p]
         count = column(stats[2 * rows:2 * rows + 8, :], d)[0:1]
         rhs = jnp.sum(total, axis=0, keepdims=True) / count
-        coef = jnp.sum(inv_all[d] * rhs, axis=1, keepdims=True)
+        coef = jnp.sum(inv_full[...] * rhs, axis=1, keepdims=True)
         coefs[...] = jnp.where(lane == d, coef, coefs[...])
         coef_wide = jnp.broadcast_to(coef, (size, LANES))
         parts = []
@@ -346,7 +380,9 @@
     dates, factors, paths = states.shape
     f32 = jnp.float32
     basis = 1 + factors + factors * (factors + 1) // 2
-    size = round_up(basis, LANES)
+    size = 2 * LANES
+    height = round_up(basis, 8)
+    assert LANES < basis < size
     slots = -(-dates // n)
     rows = round_up(factors, 8)
     dma = pltpu.SemaphoreType.DMA
@@ -363,38 +399,28 @@
                         pltpu.VMEM((n, 2 * rows + 8, LANES), f32), dma((n,)), dma((n,))],
         compiler_params=params(0), name="stats")(states, itm_flags)
 
-    grams = pl.pallas_call(
-        gram_kernel, grid=(dates,),
-        out_shape=jax.ShapeDtypeStruct((dates, size, size), f32),
-        in_specs=[pl.BlockSpec((1, factors, paths), lambda d: (d, 0, 0)),
-                  pl.BlockSpec((1, 1, paths), lambda d: (d, 0, 0)),
-                  VM],
-        out_specs=pl.BlockSpec((1, size, size), lambda d: (d, 0, 0)),
-        scratch_shapes=[pltpu.VMEM((size, paths), f32)],
-        compiler_params=pltpu.CompilerParams(vmem_limit_bytes=big), name="gram",
-    )(states, itm_flags[:, None, :], stats)
-
     system = pl.pallas_call(
-        functools.partial(reduce_kernel, n, basis),
+        functools.partial(gram_kernel, n, basis),
         out_shape=jax.ShapeDtypeStruct((slots, size, size), f32),
-        in_specs=[VM, VM], out_specs=VM,
-        scratch_shapes=[pltpu.VMEM((n, slots, size, size), f32), dma((dates,)), dma((n, slots))],
-        compiler_params=params(1), name="reduce")(grams, stats)
+        in_specs=[VM, VM, VM], out_specs=VM,
+        scratch_shapes=[pltpu.VMEM((size, paths), f32), pltpu.VMEM((dates, height, LANES), f32),
+                        pltpu.VMEM((n, slots, height, LANES), f32), dma((dates,)), dma((n, slots))],
+        compiler_params=params(1), name="gram")(states, itm_flags, stats)
 
     inverse = pl.pallas_call(
-        inverse_kernel,
-        out_shape=jax.ShapeDtypeStruct((slots, size, size), f32),
+        functools.partial(inverse_kernel, basis),
+        out_shape=jax.ShapeDtypeStruct((slots, height, LANES), f32),
         in_specs=[VM], out_specs=VM,
         scratch_shapes=[pltpu.VMEM((slots, size, size), f32)],
         compiler_params=pltpu.CompilerParams(vmem_limit_bytes=big), name="inverse")(system)
 
     flow, price, coefs = pl.pallas_call(
-        functools.partial(backward_kernel, n),
+        functools.partial(backward_kernel, n, min(3, dates)),
         out_shape=(jax.ShapeDtypeStruct((1, paths), f32), jax.ShapeDtypeStruct((1, 1), f32),
                    jax.ShapeDtypeStruct((size, LANES), f32)),
         in_specs=[VM] * 7, out_specs=(VM, VM, VM),
         scratch_shapes=[pltpu.VMEM((2, size, paths), f32), pltpu.VMEM((2, 8, paths), f32),
-                        pltpu.VMEM((dates, size, size), f32),
+                        pltpu.VMEM((dates, height, LANES), f32), pltpu.VMEM((size, size), f32),
                         pltpu.VMEM((dates, 8, size), f32), pltpu.VMEM((dates, n, 8, size), f32),
                         pltpu.VMEM((8, LANES), f32), pltpu.VMEM((n, 8, LANES), f32),
                         dma((dates, n)), dma((dates,)), dma((dates, n)), dma((dates, n)),

time: 274 us -> 178 us (0.65)
  Pallas kernels: 266 us -> 172 us
    pallas_call x4 -> x3, Pallas kernels: 253 us -> 159 us  [the longest x1 90.7 us: shards(): pl.pallas_call(functools.partial(backward_kernel, n, min(3, dates)), out_...]
where the time goes in v2:
time: 178 us
  Pallas kernels  172 us (97%)
  between operations  3.06 us (2%)
  local copies, waits for them, and re-layouts  2.89 us (2%)
    pallas_call x1, Pallas kernels, shards(): pl.pallas_call(functools.partial(backward_kernel, n, min(3, dates)), out_...  90.7 us
    pallas_call x1, Pallas kernels, shards(): pl.pallas_call(functools.partial(gram_kernel, n, basis), out_shape=jax.Sh...  39.5 us
    pallas_call x1, Pallas kernels, shards(): pl.pallas_call(functools.partial(inverse_kernel, basis), out_shape=jax.Sh...  28.3 us
    pallas_call x1, Pallas kernels, shards(): pl.pallas_call(functools.partial(stats_kernel, n), out_shape=jax.ShapeDty...  13 us

profile of v2, /device:TPU:0, one launch (start us, length us, event | category | flops | bytes accessed | tf_op | source)
XLA Modules:
  0.0 177.6 jit_solution(3740091745416982980)
XLA Ops:
  0.6 13.0 %stats.1 = f32[56,128]{1,0:T(8,128)} custom-call(f32[10,20,2048]{2,1,0:T(8,128)} %states.5, s32[10,2048]{1,0:T(8,128)} %flags.5), custom_call_target="tpu_custom_call" | custom-call | tf_op jit(solution)/shard_map/stats/pallas_call | solution.py:394
  13.6 39.5 %gram.1.system = f32[2,256,256]{2,1,0:T(8,128)} custom-call(f32[10,20,2048]{2,1,0:T(8,128)} %states.5, s32[10,2048]{1,0:T(8,128)} %flags.5, f32[56,128]{1,0:T(8,128)} %stats.1), custom_call_target="tpu_custom_call" | custom-call | tf_op jit(solution)/shard_map/gram/pallas_call | solution.py:402
  53.2 28.3 %inverse.1 = f32[2,232,128]{2,1,0:T(8,128)} custom-call(f32[2,256,256]{2,1,0:T(8,128)} %gram.1.system), custom_call_target="tpu_custom_call" | custom-call | tf_op jit(solution)/shard_map/inverse/pallas_call | solution.py:410
  82.2 90.7 %backward.1 = (f32[1,2048]{1,0:T(1,128)}, f32[1,1]{1,0:T(1,128)}, f32[256,128]{1,0:T(8,128)}) custom-call(f32[10,20,2048]{2,1,0:T(8,128)} %states.5, s32[10,2048]{1,0:T(8,128)} %flags.5, f32[1,2048]{1,0:T(1,128)} %bitcast.8, f32[1,1]{1,0:T(1,128)} %bitcast.7.strike, s32[1,2048]{1,0:T(1,128)} %bitcast.9, f32[56,128]{1,0:T(8,128)} %stats.1, f32[2,232,128]{2,1,0:T(8,128)} %inverse.1), custom_call_target="tpu_custom_call" | custom-call | tf_op jit(solution)/shard_map/backward/pallas_call | solution.py:417
  172.9 0.9 slice_bitcast_fusion
  173.8 0.7 copy.8
  174.5 1.3 copy.12

commit v3 on v2

--- a/solution.py
+++ b/solution.py
@@ -11,7 +11,7 @@
 temper_scale = 0.5
 highest = lax.Precision.HIGHEST
 LANES = 128
-BLOCK = 32
+BLOCK = LANES
 MESH = pl.DeviceIdType.MESH
 VM = pl.BlockSpec(memory_space=pltpu.VMEM)
 
@@ -48,7 +48,7 @@
     return at
 
 
-def stats_kernel(n, states, flags, out, mine, got, send_sem, recv_sem):
+def stats_kernel(n, states, flags, out, wide, mine, got, send_sem, recv_sem):
     me = lax.axis_index("path")
     dates, factors, _ = states.shape
     rows = round_up(factors, 8)
@@ -63,10 +63,11 @@
         first = jnp.where(lane == d, jnp.sum(mz, axis=1, keepdims=True), first)
         second = jnp.where(lane == d, jnp.sum(mz * z, axis=1, keepdims=True), second)
         count = jnp.where(lane == d, jnp.sum(m, axis=1, keepdims=True), count)
-    mine[...] = jnp.zeros_like(mine)
-    mine[0:factors, :] = first
-    mine[rows:rows + factors, :] = second
-    mine[2 * rows:2 * rows + 1, :] = count
+    wide[...] = jnp.zeros_like(wide)
+    wide[0:factors, :] = first
+    wide[rows:rows + factors, :] = second
+    wide[2 * rows:2 * rows + 1, :] = count
+    mine[...] = wide[...].T[0:mine.shape[0]]
     entry_barrier(me, n)
 
     def copy(o):
@@ -85,6 +86,9 @@
     total = got[0]
     for p in range(1, n):
         total = total + got[p]
+    wide[0:total.shape[0], :] = total
+    wide[total.shape[0]:, :] = jnp.zeros((LANES - total.shape[0], LANES), jnp.float32)
+    total = wide[...].T
     live = lane < dates
     count = jnp.where(live, total[2 * rows:2 * rows + 1], 1.0)
     mean = total[0:rows] / count
@@ -302,7 +306,7 @@
         for t in range(tiles):
             cols = slice(t * LANES, (t + 1) * LANES)
             acc = acc + phi[slot, :, cols] * masked[:, cols]
-        part = jnp.sum(acc.T.reshape(LANES // 8, 8, size), axis=0)
+        part = jnp.sum(acc.T, axis=0, keepdims=True)
         rhs_mine[d] = part
         for o in range(1, n):
             rhs_copy(d, o).start()
@@ -324,7 +328,7 @@
         for p in range(1, n):
             total = total + rhs_got[d, p]
         count = column(stats[2 * rows:2 * rows + 8, :], d)[0:1]
-        rhs = jnp.sum(total, axis=0, keepdims=True) / count
+        rhs = total / count
         coef = jnp.sum(inv_full[...] * rhs, axis=1, keepdims=True)
         coefs[...] = jnp.where(lane == d, coef, coefs[...])
         coef_wide = jnp.broadcast_to(coef, (size, LANES))
@@ -395,8 +399,8 @@
         functools.partial(stats_kernel, n),
         out_shape=jax.ShapeDtypeStruct((2 * rows + 8, LANES), f32),
         in_specs=[VM, VM], out_specs=VM,
-        scratch_shapes=[pltpu.VMEM((2 * rows + 8, LANES), f32),
-                        pltpu.VMEM((n, 2 * rows + 8, LANES), f32), dma((n,)), dma((n,))],
+        scratch_shapes=[pltpu.VMEM((LANES, LANES), f32), pltpu.VMEM((round_up(dates, 8), LANES), f32),
+                        pltpu.VMEM((n, round_up(dates, 8), LANES), f32), dma((n,)), dma((n,))],
         compiler_params=params(0), name="stats")(states, itm_flags)
 
     system = pl.pallas_call(
@@ -415,13 +419,13 @@
         compiler_params=pltpu.CompilerParams(vmem_limit_bytes=big), name="inverse")(system)
 
     flow, price, coefs = pl.pallas_call(
-        functools.partial(backward_kernel, n, min(3, dates)),
+        functools.partial(backward_kernel, n, min(2, dates)),
         out_shape=(jax.ShapeDtypeStruct((1, paths), f32), jax.ShapeDtypeStruct((1, 1), f32),
                    jax.ShapeDtypeStruct((size, LANES), f32)),
         in_specs=[VM] * 7, out_specs=(VM, VM, VM),
         scratch_shapes=[pltpu.VMEM((2, size, paths), f32), pltpu.VMEM((2, 8, paths), f32),
                         pltpu.VMEM((dates, height, LANES), f32), pltpu.VMEM((size, size), f32),
-                        pltpu.VMEM((dates, 8, size), f32), pltpu.VMEM((dates, n, 8, size), f32),
+                        pltpu.VMEM((dates, 1, size), f32), pltpu.VMEM((dates, n, 1, size), f32),
                         pltpu.VMEM((8, LANES), f32), pltpu.VMEM((n, 8, LANES), f32),
                         dma((dates, n)), dma((dates,)), dma((dates, n)), dma((dates, n)),
                         dma((n,)), dma((n,))],

time: 178 us -> 166 us (0.933)
  Pallas kernels: 172 us -> 159 us
    pallas_call x1, Pallas kernels: 90.7 us -> 85.8 us  [shards(): pl.pallas_call(functools.partial(backward_kernel, n, min(2, dates)), out_...]
    pallas_call x1, Pallas kernels: 28.3 us -> 23.5 us  [shards(): pl.pallas_call(functools.partial(inverse_kernel, basis), out_shape=jax.Sh...]
where the time goes in v3:
time: 166 us; the launch traced here: 165 us
  Pallas kernels  159 us (96%)
  between operations  3.06 us (2%)
  local copies, waits for them, and re-layouts  2.89 us (2%)
    pallas_call x1, Pallas kernels, shards(): pl.pallas_call(functools.partial(backward_kernel, n, min(2, dates)), out_...  85.8 us
    pallas_call x1, Pallas kernels, shards(): pl.pallas_call(functools.partial(gram_kernel, n, basis), out_shape=jax.Sh...  38.3 us
    pallas_call x1, Pallas kernels, shards(): pl.pallas_call(functools.partial(inverse_kernel, basis), out_shape=jax.Sh...  23.5 us
    pallas_call x1, Pallas kernels, shards(): pl.pallas_call(functools.partial(stats_kernel, n), out_shape=jax.ShapeDty...  11.6 us

profile of v3, /device:TPU:0, one launch (start us, length us, event | category | flops | bytes accessed | tf_op | source)
XLA Modules:
  0.0 165.2 jit_solution(15201751525872541065)
XLA Ops:
  0.6 11.6 %stats.1 = f32[56,128]{1,0:T(8,128)} custom-call(f32[10,20,2048]{2,1,0:T(8,128)} %states.5, s32[10,2048]{1,0:T(8,128)} %flags.5), custom_call_target="tpu_custom_call" | custom-call | tf_op jit(solution)/shard_map/stats/pallas_call | solution.py:398
  12.2 38.3 %gram.1.system = f32[2,256,256]{2,1,0:T(8,128)} custom-call(f32[10,20,2048]{2,1,0:T(8,128)} %states.5, s32[10,2048]{1,0:T(8,128)} %flags.5, f32[56,128]{1,0:T(8,128)} %stats.1), custom_call_target="tpu_custom_call" | custom-call | tf_op jit(solution)/shard_map/gram/pallas_call | solution.py:406
  50.5 23.5 %inverse.1 = f32[2,232,128]{2,1,0:T(8,128)} custom-call(f32[2,256,256]{2,1,0:T(8,128)} %gram.1.system), custom_call_target="tpu_custom_call" | custom-call | tf_op jit(solution)/shard_map/inverse/pallas_call | solution.py:414
  74.7 85.8 %backward.1 = (f32[1,2048]{1,0:T(1,128)}, f32[1,1]{1,0:T(1,128)}, f32[256,128]{1,0:T(8,128)}) custom-call(f32[10,20,2048]{2,1,0:T(8,128)} %states.5, s32[10,2048]{1,0:T(8,128)} %flags.5, f32[1,2048]{1,0:T(1,128)} %bitcast.8, f32[1,1]{1,0:T(1,128)} %bitcast.7.strike, s32[1,2048]{1,0:T(1,128)} %bitcast.9, f32[56,128]{1,0:T(8,128)} %stats.1, f32[2,232,128]{2,1,0:T(8,128)} %inverse.1), custom_call_target="tpu_custom_call" | custom-call | tf_op jit(solution)/shard_map/backward/pallas_call | solution.py:421
  160.5 0.9 slice_bitcast_fusion
  161.5 0.7 copy.8
  162.1 1.3 copy.12
